TPU v7x, 32 devices: a whole 2x2x4 slice. The times are simulated.
32 devices in a mesh: grp: 4 (over y, x), mem: 8 (over z, core).
Axes of the slice: x: 2, y: 2, z: 4, core: 2. Of those that a mesh axis runs over, the one named last changes fastest.
Arguments:
- values: bfloat16 [32, 8, 32, 128], P(('grp', 'mem')), may hold values from -6 to 6
- slots: int32 [32, 8, 32], P(('grp', 'mem')), may hold values from 0 to 7167
- counts: int32 [32, 8], P(('grp', 'mem')), may hold values from 0 to 32, as said below
Outputs:
- averaged: float32 [57344, 128], P('mem')
- returned: bfloat16 [32, 8, 32, 128], P(('grp', 'mem'))
Inputs may be any that keep to these rules, and one draw needn't show every extreme that they name: `counts`: every device has at least one list with exactly 32 valid entries.
All inputs are finite; a program needn't handle non-finite values.
Results may differ from a plain program's by a relative error of at most 0.0024.
Values may be sent and summed in bfloat16 or wider, within the bound.
No kernel may reach another device: no remote copies, remote signals or barrier semaphores. Data moves between devices by JAX's collectives and lax.ppermute only.
A program may use at most 64 MiB of HBM per device.

v0:
```python
import math
import jax
import jax.numpy as jnp
from jax import lax
from jax.sharding import PartitionSpec as P

BUCKET = 7168


def tiled_sums(rows_in, slot_in):
    lane_count = rows_in.shape[1]
    tile = math.gcd(BUCKET, 1024)

    def one_tile(first):
        wanted = first + lax.broadcasted_iota(jnp.int32, (tile, 1), 0)
        onehot = (wanted == slot_in[None, :]).astype(jnp.bfloat16)
        return jnp.dot(onehot, rows_in, preferred_element_type=jnp.float32)

    starts = jnp.arange(BUCKET // tile, dtype=jnp.int32) * tile
    return lax.map(one_tile, starts).reshape(BUCKET, lane_count)


def live_counts(slot_in):
    live_in = (slot_in >= 0).astype(jnp.float32)
    return jax.ops.segment_sum(live_in, jnp.maximum(slot_in, 0), num_segments=BUCKET)


def per_device(values, slots, counts):
    blocks_out = values[0]
    slot_ids = slots[0]
    list_counts = counts[0]
    members, capacity, lane_count = blocks_out.shape
    is_valid = lax.broadcasted_iota(jnp.int32, (members, capacity), 1) < list_counts[:, None]
    send_blocks = jnp.where(is_valid[:, :, None], blocks_out, jnp.zeros_like(blocks_out))
    send_slots = jnp.where(is_valid, slot_ids, -1)
    got_blocks, got_slots = (
        lax.all_to_all(send_blocks, "mem", split_axis=0, concat_axis=0, tiled=True),
        lax.all_to_all(send_slots, "mem", split_axis=0, concat_axis=0, tiled=True),
    )
    rows_in = got_blocks.reshape(members * capacity, lane_count)
    slot_in = got_slots.reshape(members * capacity)
    slot_count = None
    local_sums = tiled_sums(rows_in, slot_in)
    payload = (local_sums, live_counts(slot_in))
    reduced = lax.psum(payload, "grp")
    total_count = reduced[1]
    averaged = reduced[0] / jnp.maximum(total_count, 1.0)[:, None]
    owned_rows = jnp.take(averaged, jnp.maximum(slot_in, 0), axis=0)
    back_rows = jnp.where((slot_in >= 0)[:, None], owned_rows, 0.0).astype(jnp.bfloat16)
    back_rows = back_rows.reshape(members, capacity, lane_count)
    returned = lax.all_to_all(back_rows, "mem", split_axis=0, concat_axis=0, tiled=True)
    return (averaged, returned[None])


def solution(mesh):
    return jax.shard_map(
        per_device,
        mesh=mesh,
        in_specs=(
            P(("grp", "mem"), None, None, None),
            P(("grp", "mem"), None, None),
            P(("grp", "mem"), None),
        ),
        out_specs=(P("mem", None), P(("grp", "mem"), None, None, None)),
        check_vma=False,
    )
```

profile of v0, /device:TPU:0, one launch (start us, length us, event | category | flops | bytes accessed | tf_op | source)
XLA Modules:
  0.0 168.0 jit_solution(9887654835759522025)
XLA Ops:
  7.2 1.4 compare_select_fusion
  8.5 6.4 %all-to-all-start = ((s32[8,1,32]{2,1,0:T(1,128)}), s32[8,1,32]{2,1,0:T(1,128)S(1)}, u32[]{:S(2)}, u32[]{:S(2)}) async-start(s32[8,1,32]{2,1,0:T(1,128)} %compare_select_fusion), calls=%async_computation | async-start | bytes 8192 | tf_op jit(solution)/shard_map/all_to_all | solution.py:38
  14.9 0.7 iota_compare_fusion
  15.6 1.6 bitcast_select_fusion
  17.2 3.2 %all-to-all-done = s32[8,1,32]{2,1,0:T(1,128)S(1)} async-done(((s32[8,1,32]{2,1,0:T(1,128)}), s32[8,1,32]{2,1,0:T(1,128)S(1)}, u32[]{:S(2)}, u32[]{:S(2)}) %all-to-all-start) | async-done | bytes 1056 | tf_op jit(solution)/shard_map/all_to_all | solution.py:38
  20.4 3.4 %all-to-all-start.1 = ((bf16[8,32,128]{2,1,0:T(8,128)(2,1)}), bf16[8,32,128]{2,1,0:T(8,128)(2,1)S(1)}, u32[]{:S(2)}, u32[]{:S(2)}) async-start(bf16[8,32,128]{2,1,0:T(8,128)(2,1)} %bitcast_select_fusion), calls=%async_computation.1 | async-start | bytes 131072 | tf_op jit(solution)/shard_map/all_to_all | solution.py:37
  23.9 5.7 %all-to-all-done.1 = bf16[8,32,128]{2,1,0:T(8,128)(2,1)S(1)} async-done(((bf16[8,32,128]{2,1,0:T(8,128)(2,1)}), bf16[8,32,128]{2,1,0:T(8,128)(2,1)S(1)}, u32[]{:S(2)}, u32[]{:S(2)}) %all-to-all-start.1) | async-done | bytes 65568 | tf_op jit(solution)/shard_map/all_to_all | solution.py:37
  29.6 16.7 %while.11 = (s32[]{:T(128)}, f32[7,1024,128]{2,1,0:T(8,128)}, s32[7]{0:T(128)S(1)}, s32[8,32]{1,0:T(8,128)}, bf16[256,128]{1,0:T(8,128)(2,1)S(1)}, /*index=5*/s32[256]{0:T(256)S(1)}, s32[]{:T(128)}) while((s32[]{:T(128)}, f32[7,1024,128]{2,1,0:T(8,128)}, s32[7]{0:T(128)S(1)}, s32[8,32]{1,0:T(8,128)}, bf16[256,128]{1,0:T(8,128)(2,1)S(1)}, ...), condition=%wide.wide.region_1.2_spmd, body=%wide.wide.region_0.1_spmd.sunk | while | flops 67372032 | bytes 599645 | solution.py:20
  29.6 0.6 dynamic_slice.6
  30.2 0.6 iota_add_fusion.3
  30.8 1.2 fusion.16
  32.6 0.6 iota_add_fusion.3
  33.2 1.2 fusion.16
  34.4 0.6 dynamic_slice.6
  35.0 0.6 iota_add_fusion.3
  35.6 1.2 fusion.16
  37.4 0.6 iota_add_fusion.3
  38.0 1.2 fusion.16
  39.7 0.6 iota_add_fusion.3
  40.4 1.2 fusion.16
  42.1 0.6 iota_add_fusion.3
  42.8 1.2 fusion.16
  44.5 0.6 iota_add_fusion.3
  45.2 1.2 fusion.16
  46.4 0.6 copy-done.1
  47.2 2.1 %scatter_custom_fusion = f32[7168]{0:T(1024)S(1)} fusion(s32[256]{0:T(256)S(1)} %reshape.145, f32[256]{0:T(256)S(1)} %reshape.147, f32[]{:T(128)} %constant.16.clone.1), kind=kCustom, calls=%fused_computation.14 | custom fusion | flops 256 | bytes 28676 | tf_op jit(solution)/shard_map/scatter-add | solution.py:25
  49.3 17.7 %psum.15 = f32[7168]{0:T(1024)S(1)} all-reduce(f32[7168]{0:T(1024)S(1)} %scatter_custom_fusion), channel_id=1, replica_groups=mesh['grp'=4,'mem'=8] {'grp'}, use_global_device_ids=true, to_apply=%region_4.5 | all-reduce | flops 7168 | bytes 57344 | tf_op jit(solution)/shard_map/psum | solution.py:45
  67.0 74.6 %all-reduce.2.cloned.1.call-done = f32[7168,128]{1,0:T(8,128)} async-done(((f32[7168,128]{1,0:T(8,128)}), f32[7168,128]{1,0:T(8,128)}) %all-reduce.2.cloned.1.call-update) | async-done | bytes 3670032 | tf_op jit(solution)/shard_map/psum | solution.py:45
  141.6 5.7 %broadcast_divide_fusion = f32[7168,128]{1,0:T(8,128)} fusion(f32[7168,128]{1,0:T(8,128)} %all-reduce.2.cloned.1.call-done, f32[7168]{0:T(1024)S(1)} %broadcast_maximum_fusion), kind=kLoop, calls=%fused_computation.8 | loop fusion | flops 917504 | bytes 7368704 | tf_op jit(solution)/shard_map/div | solution.py:47
  147.3 2.8 %gather_fusion = bf16[256,128]{1,0:T(8,128)(2,1)S(1)} fusion(f32[7168,128]{1,0:T(8,128)} %broadcast_divide_fusion, s32[1024]{0:T(1024)S(1)} %pad_clamp_fusion), kind=kCustom, calls=%fused_computation | custom fusion | bytes 132096 | tf_op jit(solution)/shard_map/jit(_take)/gather | solution.py:48
  150.2 10.3 %all_to_all.19 = bf16[8,32,128]{2,1,0:T(8,128)(2,1)S(1)} all-to-all(bf16[8,32,128]{2,1,0:T(8,128)(2,1)S(1)} %select_convert_fusion), channel_id=1, replica_groups=mesh['grp'=4,'mem'=8] {'mem'}, dimensions={0} | all-to-all | bytes 131072 | tf_op jit(solution)/shard_map/all_to_all | solution.py:51
  160.5 0.6 copy.16
  (21 shorter events, 3.4 us)
Async XLA Ops:
  8.5 11.9 %all-to-all-start = ((s32[8,1,32]{2,1,0:T(1,128)}), s32[8,1,32]{2,1,0:T(1,128)S(1)}, u32[]{:S(2)}, u32[]{:S(2)}) async-start(s32[8,1,32]{2,1,0:T(1,128)} %compare_select_fusion), calls=%async_computation | async-start | bytes 8192 | tf_op jit(solution)/shard_map/all_to_all | solution.py:38
  20.4 9.2 %copy-start = (s32[8,1,32]{2,1,0:T(1,128)}, s32[8,1,32]{2,1,0:T(1,128)S(1)}, u32[]{:S(2)}) copy-start(s32[8,1,32]{2,1,0:T(1,128)S(1)} %all-to-all-done) | copy-start | bytes 3076
  20.4 9.2 %all-to-all-start.1 = ((bf16[8,32,128]{2,1,0:T(8,128)(2,1)}), bf16[8,32,128]{2,1,0:T(8,128)(2,1)S(1)}, u32[]{:S(2)}, u32[]{:S(2)}) async-start(bf16[8,32,128]{2,1,0:T(8,128)(2,1)} %bitcast_select_fusion), calls=%async_computation.1 | async-start | bytes 131072 | tf_op jit(solution)/shard_map/all_to_all | solution.py:37
  23.8 117.8 %all-reduce.2.cloned.1.call-start = ((), (), s32[]{:S(2)}) async-start(), calls=%async_computation.3 | async-start | bytes 7340032 | tf_op jit(solution)/shard_map/psum | solution.py:45
  46.3 0.7 copy-start.1
Sparse Core Ops, SparseCore 0:
  46.5 95.0 all-reduce.1
where the time goes:
time: 169 us; the launch traced here: 168 us
  waiting for transfers between devices  83.5 us (49%)
  blocking collectives  28 us (17%)
  other arithmetic  16.2 us (10%)
  between operations  14.1 us (8%)
  starting transfers between devices  9.75 us (6%)
  local copies, waits for them, and re-layouts  8.35 us (5%)
  matrix products  8.07 us (5%)
    psum x1, waiting for transfers between devices, per_device(): reduced = lax.psum(payload, 'grp')  74.6 us
    psum x1, blocking collectives, per_device(): reduced = lax.psum(payload, 'grp')  17.7 us
    all_to_all x1, blocking collectives, per_device(): lax.all_to_all(back_rows, 'mem', split_axis=0, concat_axis=0, tiled=True)  10.3 us
    dot_general x7, matrix products, one_tile(): return jnp.dot(onehot, rows_in, preferred_element_type=jnp.float32)  8.07 us
    all_to_all x1, starting transfers between devices, per_device(): lax.all_to_all(send_slots, 'mem', split_axis=0, concat_axis=0, tiled=True)  6.35 us
    div x1, other arithmetic, per_device(): averaged = reduced[0] / jnp.maximum(total_count, 1.0)[:, None]  5.72 us
    all_to_all x1, waiting for transfers between devices, per_device(): lax.all_to_all(send_blocks, 'mem', split_axis=0, concat_axis=0, tiled=True)  5.7 us
    add x7, other arithmetic, one_tile(): wanted = first + lax.broadcasted_iota(jnp.int32, (tile, 1), 0)  4.53 us
  transfers between devices with their start and end apart: 3, of which 3 were waited for; matrix products, arithmetic and copies ran while one was open for 3% of the time, Pallas kernels for 0%

commit v1 on v0

--- a/solution.py
+++ b/solution.py
@@ -5,6 +5,29 @@
 from jax.sharding import PartitionSpec as P
 
 BUCKET = 7168
+
+
+def split_up(array, dim, size):
+    lengths = array.shape
+    parts = array.reshape(*lengths[:dim], size, lengths[dim] // size, *lengths[dim + 1 :])
+    return jnp.moveaxis(parts, dim, 0)
+
+
+def laid_out(blocks, dim):
+    shape = list(blocks.shape[1:])
+    shape[dim] *= blocks.shape[0]
+    return jnp.moveaxis(blocks, 0, dim).reshape(shape)
+
+
+def sent_to_each(shard, axis, split_dim, concat_dim):
+    size, index = (lax.axis_size(axis), lax.axis_index(axis))
+    pieces = split_up(shard, split_dim, size)
+    outs = [pieces[index]]
+    for step in range(1, size):
+        sent = pieces[(index + step) % size]
+        outs.append(lax.ppermute(sent, axis, [(i, (i + step) % size) for i in range(size)]))
+    pieces = jnp.stack(outs)[(index - jnp.arange(size)) % size]
+    return laid_out(pieces, concat_dim)
 
 
 def tiled_sums(rows_in, slot_in):
@@ -35,7 +58,7 @@
     send_slots = jnp.where(is_valid, slot_ids, -1)
     got_blocks, got_slots = (
         lax.all_to_all(send_blocks, "mem", split_axis=0, concat_axis=0, tiled=True),
-        lax.all_to_all(send_slots, "mem", split_axis=0, concat_axis=0, tiled=True),
+        sent_to_each(send_slots, "mem", 0, 0),
     )
     rows_in = got_blocks.reshape(members * capacity, lane_count)
     slot_in = got_slots.reshape(members * capacity)

time: 169 us -> 178 us (1.053)
  starting transfers between devices: 9.75 us -> 15.3 us
  other arithmetic: 16.2 us -> 20.2 us
  local copies, waits for them, and re-layouts: 8.35 us -> 12.3 us
  waiting for transfers between devices: 83.5 us -> 79.9 us
    ppermute x0 -> x7, starting transfers between devices: none -> 11.9 us  [sent_to_each(): lax.ppermute(sent, axis, [(i, (i + step) % size) for i in range(size)])]
    all_to_all x1 -> x0, starting transfers between devices: 6.35 us -> none  [per_device(): lax.all_to_all(send_slots, 'mem', split_axis=0, concat_axis=0, tiled=True)]
    all_to_all x1, waiting for transfers between devices: 5.7 us -> 0.07 us  [per_device(): lax.all_to_all(send_blocks, 'mem', split_axis=0, concat_axis=0, tiled=True)]
    another operation x0 -> x7, other arithmetic: none -> 4.62 us
    psum x1, waiting for transfers between devices: 74.6 us -> 78.5 us  [per_device(): reduced = lax.psum(payload, 'grp')]
    another operation x0 -> x8, local copies, waits for them, and re-layouts: none -> 3.6 us
    all_to_all x1 -> x0, waiting for transfers between devices: 3.21 us -> none  [per_device(): lax.all_to_all(send_slots, 'mem', split_axis=0, concat_axis=0, tiled=True)]
  transfers between devices with their start and end apart: 3 -> 9, of which waited for: 3 -> 3; matrix products, arithmetic and copies ran while one was open for 3% -> 3% of each run, Pallas kernels for 0% -> 0%
where the time goes in v1:
time: 178 us
  waiting for transfers between devices  79.9 us (45%)
  blocking collectives  27.7 us (16%)
  other arithmetic  20.2 us (11%)
  starting transfers between devices  15.3 us (9%)
  between operations  14.2 us (8%)
  local copies, waits for them, and re-layouts  12.3 us (7%)
  matrix products  8.06 us (5%)
    psum x1, waiting for transfers between devices, per_device(): reduced = lax.psum(payload, 'grp')  78.5 us
    psum x1, blocking collectives, per_device(): reduced = lax.psum(payload, 'grp')  17.4 us
    ppermute x7, starting transfers between devices, sent_to_each(): lax.ppermute(sent, axis, [(i, (i + step) % size) for i in range(size)])  11.9 us
    all_to_all x1, blocking collectives, per_device(): lax.all_to_all(back_rows, 'mem', split_axis=0, concat_axis=0, tiled=True)  10.3 us
    dot_general x7, matrix products, one_tile(): return jnp.dot(onehot, rows_in, preferred_element_type=jnp.float32)  8.06 us
    div x1, other arithmetic, per_device(): averaged = reduced[0] / jnp.maximum(total_count, 1.0)[:, None]  5.72 us
    another operation x7, other arithmetic  4.62 us
    add x7, other arithmetic, one_tile(): wanted = first + lax.broadcasted_iota(jnp.int32, (tile, 1), 0)  4.53 us
  transfers between devices with their start and end apart: 9, of which 3 were waited for; matrix products, arithmetic and copies ran while one was open for 3% of the time, Pallas kernels for 0%

profile of v1, /device:TPU:0, one launch (start us, length us, event | category | flops | bytes accessed | tf_op | source)
XLA Modules:
  0.0 177.8 jit_solution(16777742917108842576)
XLA Ops:
  7.3 0.8 bitcast_select_fusion.1
  8.6 2.6 %collective-permute-start.1 = (s32[1,32]{1,0:T(1,128)S(1)}, s32[1,32]{1,0:T(1,128)S(1)}, u32[]{:S(2)}, u32[]{:S(2)}) collective-permute-start(s32[1,32]{1,0:T(1,128)S(1)} %get-tuple-element.53), channel_id=1, source_target_pairs={{0,2},{1,3},{2,4},{3,5},{4,6},{5,7},{6,0},{7,1},{8,10},{9,11},{10,... | collective-permute-start | bytes 392 | tf_op jit(solution)/shard_map/ppermute | solution.py:28
  11.2 2.5 %collective-permute-start.2 = (s32[1,32]{1,0:T(1,128)S(1)}, s32[1,32]{1,0:T(1,128)S(1)}, u32[]{:S(2)}, u32[]{:S(2)}) collective-permute-start(s32[1,32]{1,0:T(1,128)S(1)} %get-tuple-element.52), channel_id=1, source_target_pairs={{0,3},{1,4},{2,5},{3,6},{4,7},{5,0},{6,1},{7,2},{8,11},{9,12},{10,... | collective-permute-start | bytes 392 | tf_op jit(solution)/shard_map/ppermute | solution.py:28
  13.7 1.2 collective-permute-start.3
  15.0 1.2 collective-permute-start.4
  16.2 0.7 iota_compare_fusion
  16.9 1.6 bitcast_select_fusion
  18.5 3.4 %all-to-all-start = ((bf16[8,32,128]{2,1,0:T(8,128)(2,1)}), bf16[8,32,128]{2,1,0:T(8,128)(2,1)S(1)}, u32[]{:S(2)}, u32[]{:S(2)}) async-start(bf16[8,32,128]{2,1,0:T(8,128)(2,1)} %bitcast_select_fusion), calls=%async_computation | async-start | bytes 131072 | tf_op jit(solution)/shard_map/all_to_all | solution.py:60
  21.9 3.8 %collective-permute-start.5 = (s32[1,32]{1,0:T(1,128)S(1)}, s32[1,32]{1,0:T(1,128)S(1)}, u32[]{:S(2)}, u32[]{:S(2)}) collective-permute-start(s32[1,32]{1,0:T(1,128)S(1)} %get-tuple-element.49), channel_id=1, source_target_pairs={{0,6},{1,7},{2,0},{3,1},{4,2},{5,3},{6,4},{7,5},{8,14},{9,15},{10,... | collective-permute-start | bytes 392 | tf_op jit(solution)/shard_map/ppermute | solution.py:28
  25.7 1.3 collective-permute-done.5
  27.7 25.5 %while.10 = (s32[]{:T(128)}, f32[7,1024,128]{2,1,0:T(8,128)}, s32[7]{0:T(128)S(1)}, s32[8,1,32]{2,1,0:T(1,128)S(1)}, bf16[256,128]{1,0:T(8,128)(2,1)S(1)}, /*index=5*/s32[]{:T(128)}, s32[]{:T(128)}) while((s32[]{:T(128)}, f32[7,1024,128]{2,1,0:T(8,128)}, s32[7]{0:T(128)S(1)}, s32[8,1,32]{2,1,0:T(1,128)S(1)}, bf16[256,128]{1,0:T(8,128)(2,1)S(1)}, ...), condition=%wide.region_1.2_spmd, body=%wide.region_0.1_spmd.sunk | while | flops 67372032 | bytes 603253 | solution.py:43
  28.2 0.7 reduce.5
  30.2 1.2 fusion.16
  31.8 0.7 reduce.5
  33.8 1.2 fusion.16
  35.5 0.7 reduce.5
  37.5 1.1 fusion.16
  39.1 0.7 reduce.5
  40.5 0.6 iota_add_fusion.2
  41.1 1.2 fusion.16
  42.8 0.7 reduce.5
  44.8 1.2 fusion.16
  46.4 0.7 reduce.5
  48.4 1.2 fusion.16
  50.1 0.7 reduce.5
  52.0 1.2 fusion.16
  53.4 2.1 %scatter_custom_fusion = f32[7168]{0:T(1024)S(1)} fusion(s32[256]{0:T(256)S(1)} %reshape.173, f32[256]{0:T(256)S(1)} %reshape.175, f32[]{:T(128)} %constant.85.clone.1), kind=kCustom, calls=%fused_computation.13 | custom fusion | flops 256 | bytes 28676 | tf_op jit(solution)/shard_map/scatter-add | solution.py:48
  55.5 17.4 %psum.15 = f32[7168]{0:T(1024)S(1)} all-reduce(f32[7168]{0:T(1024)S(1)} %scatter_custom_fusion), channel_id=1, replica_groups=mesh['grp'=4,'mem'=8] {'grp'}, use_global_device_ids=true, to_apply=%region_4.5 | all-reduce | flops 7168 | bytes 57344 | tf_op jit(solution)/shard_map/psum | solution.py:68
  72.9 78.5 %all-reduce.2.cloned.1.call-done = f32[7168,128]{1,0:T(8,128)} async-done(((f32[7168,128]{1,0:T(8,128)}), f32[7168,128]{1,0:T(8,128)}) %all-reduce.2.cloned.1.call-update) | async-done | bytes 3670032 | tf_op jit(solution)/shard_map/psum | solution.py:68
  151.4 5.7 %broadcast_divide_fusion = f32[7168,128]{1,0:T(8,128)} fusion(f32[7168,128]{1,0:T(8,128)} %all-reduce.2.cloned.1.call-done, f32[7168]{0:T(1024)S(1)} %broadcast_maximum_fusion), kind=kLoop, calls=%fused_computation.9 | loop fusion | flops 917504 | bytes 7368704 | tf_op jit(solution)/shard_map/div | solution.py:70
  157.1 2.8 %gather_fusion.1 = bf16[256,128]{1,0:T(8,128)(2,1)S(1)} fusion(f32[7168,128]{1,0:T(8,128)} %broadcast_divide_fusion, s32[1024]{0:T(1024)S(1)} %pad_clamp_fusion), kind=kCustom, calls=%fused_computation.1 | custom fusion | bytes 132096 | tf_op jit(solution)/shard_map/jit(_take)/gather | solution.py:71
  160.0 10.3 %all_to_all.10 = bf16[8,32,128]{2,1,0:T(8,128)(2,1)S(1)} all-to-all(bf16[8,32,128]{2,1,0:T(8,128)(2,1)S(1)} %select_convert_fusion), channel_id=1, replica_groups=mesh['grp'=4,'mem'=8] {'mem'}, dimensions={0} | all-to-all | bytes 131072 | tf_op jit(solution)/shard_map/all_to_all | solution.py:74
  (53 shorter events, 14.4 us)
Async XLA Ops:
  8.0 13.9 %collective-permute-start = (s32[1,32]{1,0:T(1,128)S(1)}, s32[1,32]{1,0:T(1,128)S(1)}, u32[]{:S(2)}, u32[]{:S(2)}) collective-permute-start(s32[1,32]{1,0:T(1,128)S(1)} %get-tuple-element.54), channel_id=1, source_target_pairs={{0,1},{1,2},{2,3},{3,4},{4,5},{5,6},{6,7},{7,0},{8,9},{9,10},{10,1... | collective-permute-start | bytes 392 | tf_op jit(solution)/shard_map/ppermute | solution.py:28
  8.6 17.1 %collective-permute-start.1 = (s32[1,32]{1,0:T(1,128)S(1)}, s32[1,32]{1,0:T(1,128)S(1)}, u32[]{:S(2)}, u32[]{:S(2)}) collective-permute-start(s32[1,32]{1,0:T(1,128)S(1)} %get-tuple-element.53), channel_id=1, source_target_pairs={{0,2},{1,3},{2,4},{3,5},{4,6},{5,7},{6,0},{7,1},{8,10},{9,11},{10,... | collective-permute-start | bytes 392 | tf_op jit(solution)/shard_map/ppermute | solution.py:28
  11.2 14.5 %collective-permute-start.2 = (s32[1,32]{1,0:T(1,128)S(1)}, s32[1,32]{1,0:T(1,128)S(1)}, u32[]{:S(2)}, u32[]{:S(2)}) collective-permute-start(s32[1,32]{1,0:T(1,128)S(1)} %get-tuple-element.52), channel_id=1, source_target_pairs={{0,3},{1,4},{2,5},{3,6},{4,7},{5,0},{6,1},{7,2},{8,11},{9,12},{10,... | collective-permute-start | bytes 392 | tf_op jit(solution)/shard_map/ppermute | solution.py:28
  13.7 12.0 %collective-permute-start.3 = (s32[1,32]{1,0:T(1,128)S(1)}, s32[1,32]{1,0:T(1,128)S(1)}, u32[]{:S(2)}, u32[]{:S(2)}) collective-permute-start(s32[1,32]{1,0:T(1,128)S(1)} %get-tuple-element.51), channel_id=1, source_target_pairs={{0,4},{1,5},{2,6},{3,7},{4,0},{5,1},{6,2},{7,3},{8,12},{9,13},{10,... | collective-permute-start | bytes 392 | tf_op jit(solution)/shard_map/ppermute | solution.py:28
  15.0 10.7 %collective-permute-start.4 = (s32[1,32]{1,0:T(1,128)S(1)}, s32[1,32]{1,0:T(1,128)S(1)}, u32[]{:S(2)}, u32[]{:S(2)}) collective-permute-start(s32[1,32]{1,0:T(1,128)S(1)} %get-tuple-element.50), channel_id=1, source_target_pairs={{0,5},{1,6},{2,7},{3,0},{4,1},{5,2},{6,3},{7,4},{8,13},{9,14},{10,... | collective-permute-start | bytes 392 | tf_op jit(solution)/shard_map/ppermute | solution.py:28
  18.5 9.2 %all-to-all-start = ((bf16[8,32,128]{2,1,0:T(8,128)(2,1)}), bf16[8,32,128]{2,1,0:T(8,128)(2,1)S(1)}, u32[]{:S(2)}, u32[]{:S(2)}) async-start(bf16[8,32,128]{2,1,0:T(8,128)(2,1)} %bitcast_select_fusion), calls=%async_computation | async-start | bytes 131072 | tf_op jit(solution)/shard_map/all_to_all | solution.py:60
  21.8 129.6 %all-reduce.2.cloned.1.call-start = ((), (), s32[]{:S(2)}) async-start(), calls=%async_computation.2 | async-start | bytes 7340032 | tf_op jit(solution)/shard_map/psum | solution.py:68
  21.9 5.0 %collective-permute-start.5 = (s32[1,32]{1,0:T(1,128)S(1)}, s32[1,32]{1,0:T(1,128)S(1)}, u32[]{:S(2)}, u32[]{:S(2)}) collective-permute-start(s32[1,32]{1,0:T(1,128)S(1)} %get-tuple-element.49), channel_id=1, source_target_pairs={{0,6},{1,7},{2,0},{3,1},{4,2},{5,3},{6,4},{7,5},{8,14},{9,15},{10,... | collective-permute-start | bytes 392 | tf_op jit(solution)/shard_map/ppermute | solution.py:28
  25.7 1.3 collective-permute-start.6
Sparse Core Ops, SparseCore 0:
  53.3 98.0 all-reduce.1
